TPU v7x, 768 devices: a whole 4x8x12 slice. The times are simulated.
768 devices in a mesh: section: 24 (over z, x_lo), dp: 4 (over x_hi, core), mp: 8 (over y).
Axes of the slice: x: 4 (x_hi: 2, x_lo: 2; x = x_hi * 2 + x_lo), y: 8, z: 12, core: 2. Of those that a mesh axis runs over, the one named last changes fastest.
Arguments:
- section_in: bfloat16 [2, 24, 256, 12288], P(None, 'section', 'dp'), may hold values from -6 to 6
- out_grad: bfloat16 [2, 24, 256, 12288], P(None, 'section', 'dp'), may hold values from -1.5 to 1.5
- lengths: int32 [2, 24, 4], P(None, 'section', 'dp'), may hold values from 1 to 64, as said below
- w_in: bfloat16 [24, 2, 192, 128, 128], P('section', None, 'mp'), as said below
- w_out: bfloat16 [24, 2, 192, 128, 128], P('section', None, 'mp'), as said below
- idx_in: int32 [24, 2, 192], P('section', None, 'mp'), may hold values from 0 to 95, as said below
- idx_out: int32 [24, 2, 192], P('section', None, 'mp'), may hold values from 0 to 95, as said below
Outputs:
- passed: bfloat16 [2, 24, 256, 12288], P(None, 'section', ('dp', 'mp'))
- grads: float32 [24, 2, 8, 24, 128, 128], P(None, None, 'mp', 'section', 'dp')
Inputs may be any that keep to these rules, and one draw needn't show every extreme that they name: `lengths`: some micro-batch is full and some has a single live row. w_in[s, 1] equals w_in[23 - s, 0]: copy 1 at section s is the up relay's replica of layer 23 - s. w_out[s, 1] equals w_out[23 - s, 0]. idx_in[s, 1] equals idx_in[23 - s, 0]. idx_out[s, 1] equals idx_out[23 - s, 0].
All inputs are finite; a program needn't handle non-finite values.
Results may differ from a plain program's by a relative error of at most 0.0095.
Values may be sent and summed in bfloat16 or wider, within the bound.
A program may use at most 64 MiB of HBM per device.

v0:
```python
from functools import partial

import jax
import jax.numpy as jnp
from jax import lax
from jax.sharding import PartitionSpec as P


def from_behind(block, axis, distance):
    devices = range(lax.axis_size(axis))
    route = [(i - distance, i) for i in devices if i - distance in devices]
    return lax.ppermute(block, axis, route)


def gelu_back(pre, upstream):
    return jax.vjp(lambda value: jax.nn.gelu(value, approximate=True), pre)[1](upstream)[0]


def body(section_in, out_grad, lengths, w_in, w_out, idx_in, idx_out):
    inputs = section_in[:, 0]
    rows = inputs.shape[1]
    width = inputs.shape[2]
    block = w_in.shape[-1]
    count = width // block
    live = lax.broadcasted_iota(jnp.int32, (2, rows), 1) < lengths[:, 0, 0][:, None]
    masked = jnp.where(live[:, :, None], out_grad[:, 0], jnp.zeros((), out_grad.dtype))
    weight_in = w_in[0]
    weight_out = w_out[0]
    index_in = idx_in[0]
    index_out = idx_out[0]
    select = jax.vmap(partial(jnp.take, axis=1))
    picked = select(inputs.reshape(2, rows, count, block), index_in)
    back = select(masked.reshape(2, rows, count, block), index_out)
    pre = jnp.einsum("prjc,pjcd->prjd", picked, weight_in, preferred_element_type=jnp.float32)
    act = jax.nn.gelu(pre, approximate=True).astype(jnp.bfloat16)
    back_pre = jnp.einsum("prjd,pjcd->prjc", back, weight_out, preferred_element_type=jnp.float32)
    grad_pre = gelu_back(pre, back_pre).astype(jnp.bfloat16)
    terms = jnp.einsum("prjd,pjcd->prjc", grad_pre, weight_in, preferred_element_type=jnp.float32)
    share = rows // lax.axis_size("mp")
    first = lax.axis_index("mp") * share
    onehot = jax.nn.one_hot(index_in, count, dtype=jnp.float32)
    local_terms = jnp.einsum(
        "prjc,pjb->prbc", terms, onehot, precision=lax.Precision.HIGHEST
    ).reshape(2, rows, width)
    summed = lax.psum(local_terms.astype(jnp.bfloat16), "mp").astype(jnp.float32)
    summed = lax.dynamic_slice_in_dim(summed, first, share, 1)
    own_rows = lax.dynamic_slice_in_dim(masked, first, share, 1)
    result = (own_rows.astype(jnp.float32) + summed).astype(jnp.bfloat16)
    from_next = from_behind(result[0], "section", -1)
    from_prev = from_behind(result[1], "section", 1)
    passed = jnp.stack([from_next, from_prev], axis=0)[:, None]
    grad_in = jnp.einsum("prjc,prjd->pjcd", picked, grad_pre, preferred_element_type=jnp.float32)
    grad_out = jnp.einsum("prjc,prjd->pjcd", act, back, preferred_element_type=jnp.float32)
    stacked = jnp.stack([grad_in, grad_out], axis=1)
    reduced = lax.psum_scatter(
        stacked.astype(jnp.bfloat16), "dp", scatter_dimension=3, tiled=True
    ).astype(jnp.float32)
    moved = lax.all_to_all(
        reduced[None].astype(jnp.bfloat16), "section", split_axis=3, concat_axis=0, tiled=True
    ).astype(jnp.float32)
    total = moved[:, 0] + jnp.flip(moved[:, 1], 0)
    return (passed, total[:, :, None])


def solution(mesh):
    placed = (
        P(None, "section", "dp", None),
        P(None, "section", "dp", None),
        P(None, "section", "dp"),
        P("section", None, "mp", None, None),
        P("section", None, "mp", None, None),
        P("section", None, "mp"),
        P("section", None, "mp"),
    )
    return jax.shard_map(
        body,
        mesh=mesh,
        in_specs=placed,
        out_specs=(
            P(None, "section", ("dp", "mp"), None),
            P(None, None, "mp", "section", "dp", None),
        ),
        check_vma=False,
    )
```

profile of v0, /device:TPU:1, one launch (start us, length us, event | category | flops | bytes accessed | tf_op | source)
XLA Modules:
  0.0 207.1 jit_solution(10365697554272115801)
XLA Ops:
  8.0 0.0 copy-start
  8.0 0.0 all-reduce.2.cloned.1.call-start
  8.1 0.8 compare_and_fusion
  8.9 0.7 bitcast_or_fusion
  9.6 0.7 iota_compare_fusion.1
  10.3 0.1 reshape.84
  10.4 0.1 reshape.79
  10.5 2.6 %copy.29 = bf16[16,8,96,128]{3,2,1,0:T(8,128)(2,1)S(1)} copy(bf16[16,8,96,128]{3,1,2,0:T(8,128)(2,1)} %bitcast.133) | data formatting | bytes 6291456
  13.1 0.0 copy-start.1
  13.1 2.9 %copy.21 = bf16[2,64,96,128]{3,1,2,0:T(8,128)(2,1)} copy(bf16[2,64,96,128]{3,2,1,0:T(8,128)(2,1)S(1)} %bitcast.128) | data formatting | bytes 6291456 | tf_op jit(solution)/shard_map/reshape;squeeze | solution.py:32
  16.0 2.3 %copy.28 = bf16[16,8,96,128]{3,2,1,0:T(8,128)(2,1)} copy(bf16[16,8,96,128]{3,1,2,0:T(8,128)(2,1)S(1)} %bitcast.132) | data formatting | bytes 6291456
  18.3 2.8 %gather_fusion.1 = bf16[48,64,128]{2,1,0:T(8,128)(2,1)S(1)} fusion(bf16[2,64,96,128]{3,1,2,0:T(8,128)(2,1)} %copy.21, s32[48]{0:T(128)S(1)} %reshape.84), kind=kCustom, calls=%fused_computation.1.clone | custom fusion | bytes 1573248 | tf_op jit(solution)/shard_map/vmap(jit(_take))/gather | solution.py:32
  21.1 4.6 %copy_select_fusion = bf16[2,64,96,128]{3,1,2,0:T(8,128)(2,1)} fusion(bf16[2,64,96,128]{3,2,1,0:T(8,128)(2,1)} %bitcast.127, pred[2,64]{1,0:T(4,128)(4,1)S(1)} %iota_compare_fusion.1), kind=kLoop, calls=%fused_computation.3 | loop fusion | flops 1572864 | bytes 6291584 | tf_op jit(solution)/shard_map/jit(_where)/select_n | solution.py:26
  25.7 3.7 %gather_fusion = bf16[48,64,128]{2,1,0:T(8,128)(2,1)} fusion(bf16[2,64,96,128]{3,1,2,0:T(8,128)(2,1)} %copy_select_fusion, s32[48]{0:T(128)S(1)} %reshape.79), kind=kCustom, calls=%fused_computation.clone | custom fusion | bytes 1573248 | tf_op jit(solution)/shard_map/vmap(jit(_take))/gather | solution.py:33
  29.4 0.6 fusion.12
  30.0 0.0 copy-start.2
  30.0 1.1 copy-done.2
  31.1 0.0 copy-done.4
  31.1 0.1 copy-done.7
  31.2 1.5 fusion.6
  32.8 0.0 copy-start.6
  32.8 1.2 fusion.18
  34.0 4.3 %convert_bitcast_fusion = bf16[2,64,96,128]{3,2,1,0:T(8,128)(2,1)} fusion(f32[2,64,24,128]{3,1,2,0:T(8,128)S(1)} %fusion.18, s32[2,24]{1,0:T(2,128)S(1)} %bitcast.139), kind=kOutput, calls=%fused_computation.4 | convolution fusion | flops 454562304 | bytes 4718784 | tf_op jit(solution)/shard_map/prjc,pjb->prbc/dot_general | solution.py:42
  38.3 5.7 %convert_element_type.56 = bf16[2,64,12288]{2,1,0:T(8,128)(2,1)} reshape(bf16[2,64,96,128]{3,2,1,0:T(8,128)(2,1)} %convert_bitcast_fusion) | data formatting | bytes 6291456 | tf_op jit(solution)/shard_map/convert_element_type | solution.py:45
  43.9 0.0 all-reduce.2.cloned.1.call-update
  44.0 0.0 reduce-scatter.2.cloned.1.call-start
  44.0 0.0 copy-start.5
  44.0 0.7 fusion.21
  44.8 0.7 copy-done.3
  45.4 0.2 copy-done.5
  45.6 0.9 fusion.22
  46.6 2.0 pad_maximum_fusion
  48.5 0.0 reduce-scatter.2.cloned.1.call-update
  48.6 0.1 constant_dynamic-slice_fusion
  48.6 104.5 %all-reduce.2.cloned.1.call-done = bf16[2,64,12288]{2,1,0:T(8,128)(2,1)} async-done(((bf16[2,64,12288]{2,1,0:T(8,128)(2,1)}), bf16[2,64,12288]{2,1,0:T(8,128)(2,1)}) %all-reduce.2.cloned.1.call-update) | async-done | bytes 3145744 | tf_op jit(solution)/shard_map/psum | solution.py:45
  153.2 1.3 add_convert_fusion
  154.5 0.0 reduce-scatter.2.cloned.1.call-done
  154.5 2.1 %copy.23 = bf16[1,2,2,24,32,128]{5,4,1,2,0,3:T(8,128)(2,1)} copy(bf16[1,2,2,24,32,128]{5,4,3,1,2,0:T(8,128)(2,1)} %bitcast.134) | data formatting | bytes 1572864 | tf_op jit(solution)/shard_map/convert_element_type | solution.py:59
  156.6 11.0 %all-to-all-start = ((bf16[1,2,2,24,32,128]{5,4,1,2,0,3:T(8,128)(2,1)}), bf16[1,2,2,24,32,128]{5,4,1,2,0,3:T(8,128)(2,1)S(1)}, u32[]{:S(2)}, u32[]{:S(2)}) async-start(bf16[1,2,2,24,32,128]{5,4,1,2,0,3:T(8,128)(2,1)} %copy.23), calls=%async_computation.1 | async-start | bytes 1572864 | tf_op jit(solution)/shard_map/all_to_all | solution.py:58
  167.7 1.3 collective-permute-start
  169.0 4.0 %collective-permute-start.1 = (bf16[8,12288]{1,0:T(8,128)(2,1)S(1)}, bf16[8,12288]{1,0:T(8,128)(2,1)S(1)}, u32[]{:S(2)}, u32[]{:S(2)}) collective-permute-start(bf16[8,12288]{1,0:T(8,128)(2,1)S(1)} %get-tuple-element.12), channel_id=1, source_target_pairs={{0,32},{32,64},{64,96},{96,128},{128,160},{160,192},{192,224},{224... | collective-permute-start | bytes 589832 | tf_op jit(solution)/shard_map/ppermute | solution.py:12
  173.0 3.0 %collective-permute-done = bf16[8,12288]{1,0:T(8,128)(2,1)S(1)} collective-permute-done((bf16[8,12288]{1,0:T(8,128)(2,1)S(1)}, bf16[8,12288]{1,0:T(8,128)(2,1)S(1)}, u32[]{:S(2)}, u32[]{:S(2)}) %collective-permute-start) | collective-permute-done | bytes 196640 | tf_op jit(solution)/shard_map/ppermute | solution.py:12
  176.0 1.4 collective-permute-done.1
  177.4 0.8 maximum_bitcast_fusion
  178.2 20.2 %all-to-all-done = bf16[1,2,2,24,32,128]{5,4,1,2,0,3:T(8,128)(2,1)S(1)} async-done(((bf16[1,2,2,24,32,128]{5,4,1,2,0,3:T(8,128)(2,1)}), bf16[1,2,2,24,32,128]{5,4,1,2,0,3:T(8,128)(2,1)S(1)}, u32[]{:S(2)}, u32[]{:S(2)}) %all-to-all-start) | async-done | bytes 786464 | tf_op jit(solution)/shard_map/all_to_all | solution.py:58
  198.4 0.2 convert_bitcast_fusion.1
  198.6 0.1 slice_bitcast_fusion
  198.6 1.0 fusion.27
  (7 shorter events, 0.0 us)
Async XLA Ops:
  8.0 21.4 %copy-start = (bf16[1,2,24,128,128]{4,3,2,1,0:T(8,128)(2,1)S(1)}, bf16[1,2,24,128,128]{4,3,2,1,0:T(8,128)(2,1)}, u32[]{:S(2)}) copy-start(bf16[1,2,24,128,128]{4,3,2,1,0:T(8,128)(2,1)} %param.12) | copy-start | bytes 4718596
  8.0 145.2 %all-reduce.2.cloned.1.call-start = ((), (), s32[]{:S(2)}) async-start(), calls=%async_computation.2 | async-start | bytes 6291456 | tf_op jit(solution)/shard_map/psum | solution.py:45
  13.1 2.9 %copy-start.1 = (bf16[2,1,64,12288]{3,2,1,0:T(8,128)(2,1)S(1)}, bf16[2,1,64,12288]{3,2,1,0:T(8,128)(2,1)}, u32[]{:S(2)}) copy-start(bf16[2,1,64,12288]{3,2,1,0:T(8,128)(2,1)} %param.10) | copy-start | bytes 9437188
  29.4 1.8 copy-start.4
  29.4 1.9 copy-start.7
  30.0 1.2 copy-start.2
  32.8 1.2 copy-start.6
  44.0 110.5 %reduce-scatter.2.cloned.1.call-start = ((), (), s32[]{:S(2)}) async-start(), calls=%async_computation.3 | async-start | bytes 3932160 | tf_op jit(solution)/shard_map/reduce_scatter | solution.py:55
  44.0 1.4 copy-start.3
  44.0 1.6 copy-start.5
  156.6 41.7 %all-to-all-start = ((bf16[1,2,2,24,32,128]{5,4,1,2,0,3:T(8,128)(2,1)}), bf16[1,2,2,24,32,128]{5,4,1,2,0,3:T(8,128)(2,1)S(1)}, u32[]{:S(2)}, u32[]{:S(2)}) async-start(bf16[1,2,2,24,32,128]{5,4,1,2,0,3:T(8,128)(2,1)} %copy.23), calls=%async_computation.1 | async-start | bytes 1572864 | tf_op jit(solution)/shard_map/all_to_all | solution.py:58
  167.7 8.3 %collective-permute-start = (bf16[8,12288]{1,0:T(8,128)(2,1)S(1)}, bf16[8,12288]{1,0:T(8,128)(2,1)S(1)}, u32[]{:S(2)}, u32[]{:S(2)}) collective-permute-start(bf16[8,12288]{1,0:T(8,128)(2,1)S(1)} %get-tuple-element.11), channel_id=1, source_target_pairs={{32,0},{64,32},{96,64},{128,96},{160,128},{192,160},{224,192},{256... | collective-permute-start | bytes 589832 | tf_op jit(solution)/shard_map/ppermute | solution.py:12
  169.0 8.4 %collective-permute-start.1 = (bf16[8,12288]{1,0:T(8,128)(2,1)S(1)}, bf16[8,12288]{1,0:T(8,128)(2,1)S(1)}, u32[]{:S(2)}, u32[]{:S(2)}) collective-permute-start(bf16[8,12288]{1,0:T(8,128)(2,1)S(1)} %get-tuple-element.12), channel_id=1, source_target_pairs={{0,32},{32,64},{64,96},{96,128},{128,160},{160,192},{192,224},{224... | collective-permute-start | bytes 589832 | tf_op jit(solution)/shard_map/ppermute | solution.py:12
Sparse Core Ops, SparseCore 0:
  44.1 109.0 all-reduce.1
Sparse Core Ops, SparseCore 1:
  48.7 68.1 reduce-scatter.1
where the time goes:
time: 209 us; the launch traced here: 207 us
  waiting for transfers between devices  129 us (62%)
  local copies, waits for them, and re-layouts  24.5 us (12%)
  starting transfers between devices  16.4 us (8%)
  between operations  15.6 us (7%)
  other arithmetic  12.2 us (6%)
  matrix products  9.24 us (4%)
    psum x1, waiting for transfers between devices, body(): lax.psum(local_terms.astype(jnp.bfloat16), 'mp').astype(jnp.float32)  105 us
    all_to_all x1, waiting for transfers between devices, body(): lax.all_to_all(reduced[None].astype(jnp.bfloat16), 'section', split_axis=...  20.2 us
    all_to_all x1, starting transfers between devices, body(): lax.all_to_all(reduced[None].astype(jnp.bfloat16), 'section', split_axis=...  11 us
    unnamed x18, local copies, waits for them, and re-layouts  7.12 us
    convert_element_type x1, local copies, waits for them, and re-layouts, body(): local_terms.astype(jnp.bfloat16)  5.65 us
    ppermute x2, starting transfers between devices, from_behind(): return lax.ppermute(block, axis, route)  5.29 us
    select_n x1, other arithmetic, body(): jnp.where(live[:, :, None], out_grad[:, 0], jnp.zeros((), out_grad.dtype))  4.63 us
    ppermute x2, waiting for transfers between devices, from_behind(): return lax.ppermute(block, axis, route)  4.44 us
  transfers between devices with their start and end apart: 5, of which 4 were waited for; matrix products, arithmetic and copies ran while one was open for 3% of the time, Pallas kernels for 0%

commit v1 on v0

v1 whole, which is shorter than its diff:
```python
import functools

import jax
import jax.numpy as jnp
from jax import lax
from jax.experimental import pallas as pl
from jax.experimental.pallas import tpu as pltpu
from jax.sharding import PartitionSpec as P

MESH = pl.DeviceIdType.MESH
F32 = jnp.float32
BF16 = jnp.bfloat16
ROOT = 0.7978845608028654
CUBIC = 0.044715


def contract(a, b, da, db):
    return lax.dot_general(a, b, (((da,), (db,)), ((), ())), preferred_element_type=F32)


def kernel(
    nz, nmp,
    len_ref, ii_ref, io_ref, x_hbm, g_hbm, wi_hbm, wo_hbm,
    passed_ref, grads_ref,
    x0, x1, g0, g1, wiv, wov, part, from_core, pair, from_x, ready, landed,
    terms, got, code, codes, dx, dx_in,
    in_sem, a_send, a_recv, b_send, b_recv, c_send, c_recv,
    t_send, t_recv, k_send, k_recv, d_send, d_recv,
):
    ns = 2 * nz
    s = lax.axis_index("section")
    r = lax.axis_index("dp")
    m = lax.axis_index("mp")
    z, xl = s // 2, lax.rem(s, 2)
    xh, c = r // 2, lax.rem(r, 2)
    rows, width = x0.shape
    count = width // 128
    xs, gs = (x0, x1), (g0, g1)

    def dev(section, dp, mp):
        return {"section": section, "dp": dp, "mp": mp}

    partner = dev(s, 2 * xh + (1 - c), m)
    across = dev(s, 2 * (1 - xh) + c, m)
    sides = [dev(2 * z + (1 - xl), 2 * h + c, m) for h in range(2)]
    down = dev(lax.rem(s + ns - 1, ns), r, m)
    up = dev(lax.rem(s + 1, ns), r, m)

    def along_z(k):
        half = (k + 1) // 2
        to = jnp.where(lax.rem(k, 2) == 0, z + (nz // 2 - k // 2), z - (nz // 2 - half))
        return lax.rem(to + nz, nz)

    def along_y(k):
        half = (k + 1) // 2
        to = jnp.where(lax.rem(k, 2) == 0, m + (nmp // 2 - k // 2), m - (nmp // 2 - half))
        return lax.rem(to + nmp, nmp)

    barrier = pltpu.get_barrier_semaphore()

    def greet(target):
        pl.semaphore_signal(barrier, inc=1, device_id=target, device_id_type=MESH)

    for target in [partner, across, sides[0], sides[1], down, up]:
        greet(target)

    @pl.loop(0, nz - 1)
    def _(k):
        greet(dev(2 * along_z(k) + xl, r, m))

    @pl.loop(0, nmp - 1)
    def _(k):
        greet(dev(s, r, along_y(k)))

    loads = []
    for p in range(2):
        loads.append([
            pltpu.make_async_copy(x_hbm.at[p], xs[p], in_sem.at[p, 0]),
            pltpu.make_async_copy(wi_hbm.at[p], wiv.at[p], in_sem.at[p, 1]),
            pltpu.make_async_copy(g_hbm.at[p], gs[p], in_sem.at[p, 2]),
            pltpu.make_async_copy(wo_hbm.at[p], wov.at[p], in_sem.at[p, 3]),
        ])
        for load in loads[p]:
            load.start()

    wide = code.shape[1]
    lane = lax.broadcasted_iota(jnp.int32, (8, wide), 1)
    relay = lax.broadcasted_iota(jnp.int32, (8, wide), 0)
    value = jnp.full((8, wide), -1, jnp.int32)
    for j in range(2 * nz):
        chosen = jnp.where(relay == 0, ii_ref[0, j], ii_ref[1, j])
        value = jnp.where(lane // 8 == j, chosen * 8 + lane % 8, value)
    code[...] = value

    def compute(p):
        live = lax.broadcasted_iota(jnp.int32, (rows, 128), 0) < len_ref[p]

        @pl.loop(0, nz)
        def _(q):
            kept = []
            for u in range(2):
                j = 2 * q + u
                at_in = ii_ref[p, j] * 128
                at_out = io_ref[p, j] * 128
                x = xs[p][:, pl.ds(at_in, 128)]
                back = jnp.where(live, gs[p][:, pl.ds(at_out, 128)].astype(F32), 0.0).astype(BF16)
                wi = wiv[p, j]
                wo = wov[p, j]
                pre = contract(x, wi, 1, 0)
                back_pre = contract(back, wo, 1, 1)
                square = pre * pre
                t = jnp.tanh(ROOT * (pre + CUBIC * (square * pre)))
                half = 0.5 * (1.0 + t)
                act = (pre * half).astype(BF16)
                slope = half + (0.5 * pre) * (1.0 - t * t) * (ROOT * (1.0 + (3.0 * CUBIC) * square))
                grad = (back_pre * slope).astype(BF16)
                kept.append(contract(grad, wi, 1, 1))
                g_in = contract(x, grad, 0, 0).astype(BF16)
                g_out = contract(act, back, 0, 0).astype(BF16)
                for h in range(2):
                    for d in range(2):
                        lo = 32 * (2 * h + d)
                        part[2 * p, d, u, h, q] = g_in[lo:lo + 32]
                        part[2 * p + 1, d, u, h, q] = g_out[lo:lo + 32]
            at = pl.multiple_of(16 * q, 16)
            for y in range(nmp):
                both = jnp.concatenate([kept[0][8 * y:8 * y + 8], kept[1][8 * y:8 * y + 8]], axis=0)
                terms[p, y, pl.ds(at, 16), :] = both.astype(BF16)

    def remote(src, dst, send, recv, target):
        return pltpu.make_async_remote_copy(
            src_ref=src, dst_ref=dst, send_sem=send, recv_sem=recv,
            device_id=target, device_id_type=MESH)

    def copy_a(k):
        return remote(part.at[k, 1 - c], from_core.at[k], a_send.at[k], a_recv.at[k], partner)

    def copies_b(k):
        out = [remote(pair.at[k, xl, 1 - xh], from_x.at[k, 0], b_send.at[k, 0], b_recv.at[k, 0], across)]
        for h in range(2):
            out.append(remote(pair.at[k, 1 - xl, h], from_x.at[k, 1 + xh],
                              b_send.at[k, 1 + h], b_recv.at[k, 1 + xh], sides[h]))
        return out

    def wait_b(k):
        for i in range(3):
            remote(from_x.at[k, i], from_x.at[k, i], b_send.at[k, i], b_recv.at[k, i], across).wait_recv()

    def copy_c(k, to):
        return remote(ready.at[k, to], landed.at[k, z], c_send.at[k, to], c_recv.at[k, z],
                      dev(2 * to + xl, r, m))

    def arrived_c(k, origin):
        return remote(landed.at[k, origin], landed.at[k, origin], c_send.at[k, origin], c_recv.at[k, origin], partner)

    def copy_t(p, to):
        return remote(terms.at[p, to], got.at[p, m], t_send.at[p, to], t_recv.at[p, m], dev(s, r, to))

    def arrived_t(p, origin):
        return remote(got.at[p, origin], got.at[p, origin], t_send.at[p, origin], t_recv.at[p, origin], partner)

    def copy_k(to):
        return remote(code, codes.at[m], k_send.at[to], k_recv.at[m], dev(s, r, to))

    def arrived_k(origin):
        return remote(codes.at[origin], codes.at[origin], k_send.at[origin], k_recv.at[origin], partner)

    def send_terms(p):
        @pl.loop(0, nmp - 1)
        def _(k):
            copy_t(p, along_y(k)).start()
        got[p, m] = terms[p, m]

    def add_pair(k):
        copy_a(k).wait_recv()

        @pl.loop(0, nz)
        def _(q):
            for u in range(2):
                for h in range(2):
                    pair[k, u, h, q] = (part[k, c, u, h, q].astype(F32) + from_core[k, u, h, q].astype(F32)).astype(BF16)
        for copy in copies_b(k):
            copy.start()

    def add_x(k):
        wait_b(k)

        @pl.loop(0, nz)
        def _(q):
            ready[k, q, xl] = (pair[k, xl, xh, q].astype(F32) + from_x[k, 0, q].astype(F32)).astype(BF16)
            ready[k, q, 1 - xl] = (from_x[k, 1, q].astype(F32) + from_x[k, 2, q].astype(F32)).astype(BF16)

        @pl.loop(0, nz - 1)
        def _(i):
            copy_c(k, along_z(i)).start()
        landed[k, z] = ready[k, z]

    for load in loads[0]:
        load.wait()
    compute(0)
    pl.semaphore_wait(barrier, 6 + (nz - 1) + (nmp - 1))
    copy_a(0).start()
    copy_a(1).start()

    @pl.loop(0, nmp - 1)
    def _(k):
        copy_k(along_y(k)).start()
    codes[m] = code[...]
    send_terms(0)

    for load in loads[1]:
        load.wait()
    compute(1)
    copy_a(2).start()
    copy_a(3).start()
    send_terms(1)

    for k in range(4):
        add_pair(k)
    for k in range(4):
        add_x(k)

    @pl.loop(0, nmp - 1)
    def _(i):
        arrived_k(along_y(i)).wait_recv()

    first = pl.multiple_of(16 * (m // 2), 16)
    odd = lax.rem(m, 2) == 1
    row = lax.broadcasted_iota(jnp.int32, (8, 128), 0) + 8 * m
    span = 8 * ns
    tile = 8 * count // 6 if (8 * count) % 96 == 0 else 8 * count
    for p in range(2):
        @pl.loop(0, nmp - 1)
        def _(i):
            arrived_t(p, along_y(i)).wait_recv()

        @pl.loop(0, 8 * count // tile)
        def _(i):
            base = i * tile
            place = lax.broadcasted_iota(jnp.int32, (tile, span), 0) + base
            total = jnp.zeros((tile, 128), F32)
            for y in range(nmp):
                hot = (place == codes[y, p:p + 1, :span]).astype(F32).astype(BF16)
                total = total + contract(hot, got[p, y], 1, 0)
            for b in range(tile // 8):
                at = pl.multiple_of(base * 16 + b * 128, 128)
                mine = gs[p][pl.ds(first, 16), pl.ds(at, 128)].astype(F32)
                mine = jnp.where(odd, mine[8:16], mine[0:8])
                mine = jnp.where(row < len_ref[p], mine, 0.0)
                dx[p, :, pl.ds(at, 128)] = (mine + total[8 * b:8 * b + 8]).astype(BF16)

        remote(dx.at[p], dx_in.at[p], d_send.at[p], d_recv.at[p], (down, up)[p]).start()

    for k in range(4):
        @pl.loop(0, nz - 1)
        def _(i):
            arrived_c(k, along_z(i)).wait_recv()

    @pl.loop(0, nz)
    def _(q):
        for kind in range(2):
            for u in range(2):
                grads_ref[2 * q + u, kind] = (landed[kind, q, u].astype(F32)
                                              + landed[2 + kind, nz - 1 - q, 1 - u].astype(F32))

    for p in range(2):
        remote(dx.at[p], dx_in.at[p], d_send.at[p], d_recv.at[p], (down, up)[p]).wait_recv()
        edge = s == (ns - 1 if p == 0 else 0)
        taken = dx_in[p]
        passed_ref[p] = jnp.where(edge, jnp.zeros_like(taken), taken)

    for k in range(4):
        copy_a(k).wait_send()
        for copy in copies_b(k):
            copy.wait_send()

        @pl.loop(0, nz - 1)
        def _(i):
            copy_c(k, along_z(i)).wait_send()

    @pl.loop(0, nmp - 1)
    def _(i):
        copy_k(along_y(i)).wait_send()
        for p in range(2):
            copy_t(p, along_y(i)).wait_send()
    for p in range(2):
        remote(dx.at[p], dx_in.at[p], d_send.at[p], d_recv.at[p], (down, up)[p]).wait_send()


def body(section_in, out_grad, lengths, w_in, w_out, idx_in, idx_out):
    x = section_in[:, 0]
    g = out_grad[:, 0]
    rows, width = x.shape[1:]
    nf = w_in.shape[2]
    nz = lax.axis_size("section") // 2
    nmp = lax.axis_size("mp")
    wide = -(-8 * nf // 128) * 128
    quad = (2, 2, nz, 32, 128)
    dma = pltpu.SemaphoreType.DMA
    smem = pl.BlockSpec(memory_space=pltpu.SMEM)
    anywhere = pl.BlockSpec(memory_space=pl.ANY)
    vmem = pl.BlockSpec(memory_space=pltpu.VMEM)
    passed, grads = pl.pallas_call(
        functools.partial(kernel, nz, nmp),
        out_shape=(
            jax.ShapeDtypeStruct((2, 8, width), BF16),
            jax.ShapeDtypeStruct((nf, 2, 32, 128), F32),
        ),
        in_specs=[smem] * 3 + [anywhere] * 4,
        out_specs=(vmem, vmem),
        scratch_shapes=[
            pltpu.VMEM((rows, width), BF16),
            pltpu.VMEM((rows, width), BF16),
            pltpu.VMEM((rows, width), BF16),
            pltpu.VMEM((rows, width), BF16),
            pltpu.VMEM((2, nf, 128, 128), BF16),
            pltpu.VMEM((2, nf, 128, 128), BF16),
            pltpu.VMEM((4, 2) + quad, BF16),
            pltpu.VMEM((4,) + quad, BF16),
            pltpu.VMEM((4,) + quad, BF16),
            pltpu.VMEM((4, 3, nz, 32, 128), BF16),
            pltpu.VMEM((4, nz, 2, 32, 128), BF16),
            pltpu.VMEM((4, nz, 2, 32, 128), BF16),
            pltpu.VMEM((2, nmp, 8 * nf, 128), BF16),
            pltpu.VMEM((2, nmp, 8 * nf, 128), BF16),
            pltpu.VMEM((8, wide), jnp.int32),
            pltpu.VMEM((nmp, 8, wide), jnp.int32),
            pltpu.VMEM((2, 8, width), BF16),
            pltpu.VMEM((2, 8, width), BF16),
            dma((2, 4)), dma((4,)), dma((4,)), dma((4, 3)), dma((4, 3)),
            dma((4, nz)), dma((4, nz)), dma((2, nmp)), dma((2, nmp)),
            dma((nmp,)), dma((nmp,)), dma((2,)), dma((2,)),
        ],
        compiler_params=pltpu.CompilerParams(
            collective_id=0, has_side_effects=True, vmem_limit_bytes=60 * 2**20),
    )(lengths[:, 0, 0], idx_in[0], idx_out[0], x, g, w_in[0], w_out[0])
    return passed[:, None], grads[:, :, None, None]


def solution(mesh):
    placed = (
        P(None, "section", "dp", None),
        P(None, "section", "dp", None),
        P(None, "section", "dp"),
        P("section", None, "mp", None, None),
        P("section", None, "mp", None, None),
        P("section", None, "mp"),
        P("section", None, "mp"),
    )
    return jax.shard_map(
        body,
        mesh=mesh,
        in_specs=placed,
        out_specs=(
            P(None, "section", ("dp", "mp"), None),
            P(None, None, "mp", "section", "dp", None),
        ),
        check_vma=False,
    )
```

time: 209 us -> 76.4 us (0.37)
  waiting for transfers between devices: 129 us -> 0 us
  Pallas kernels: 0 us -> 71.7 us
  local copies, waits for them, and re-layouts: 24.5 us -> 3.85 us
  starting transfers between devices: 16.4 us -> 0 us
  between operations: 15.6 us -> 0.64 us
  other arithmetic: 12.2 us -> 0 us
  matrix products: 9.24 us -> 0 us
    psum x1 -> x0, waiting for transfers between devices: 105 us -> none  [body(): lax.psum(local_terms.astype(jnp.bfloat16), 'mp').astype(jnp.float32)]
    pallas_call x0 -> x1, Pallas kernels: none -> 71.7 us  [body(): pl.pallas_call(functools.partial(kernel, nz, nmp), out_shape=(jax.ShapeDt...]
    all_to_all x1 -> x0, waiting for transfers between devices: 20.2 us -> none  [body(): lax.all_to_all(reduced[None].astype(jnp.bfloat16), 'section', split_axis=...]
    all_to_all x1 -> x0, starting transfers between devices: 11 us -> none  [body(): lax.all_to_all(reduced[None].astype(jnp.bfloat16), 'section', split_axis=...]
    dot_general x6 -> x0, matrix products: 9.24 us -> none  [the longest x1 4.33 us: body(): jnp.einsum('prjc,pjb->prbc', terms, onehot, precision=lax.Precision.HIGHEST)]
    convert_element_type x2 -> x0, local copies, waits for them, and re-layouts: 7.78 us -> none  [the longest x1 5.65 us: body(): local_terms.astype(jnp.bfloat16)]
    gather x4 -> x0, local copies, waits for them, and re-layouts: 6.58 us -> none  [the longest x2 3.73 us: body(): back = select(masked.reshape(2, rows, count, block), index_out)]
    ppermute x2 -> x0, starting transfers between devices: 5.29 us -> none  [from_behind(): return lax.ppermute(block, axis, route)]
  transfers between devices with their start and end apart: 5 -> 0, of which waited for: 4 -> 0; matrix products, arithmetic and copies ran while one was open for 3% -> 0% of each run, Pallas kernels for 0% -> 0%
where the time goes in v1:
time: 76.4 us; the launch traced here: 76.2 us
  Pallas kernels  71.7 us (94%)
  local copies, waits for them, and re-layouts  3.85 us (5%)
    pallas_call x1, Pallas kernels, body(): pl.pallas_call(functools.partial(kernel, nz, nmp), out_shape=(jax.ShapeDt...  71.7 us
    unnamed x2, local copies, waits for them, and re-layouts  3.85 us

profile of v1, /device:TPU:1, one launch (start us, length us, event | category | flops | bytes accessed | tf_op | source)
XLA Modules:
  0.0 76.2 jit_solution(7388124740675689990)
XLA Ops:
  0.6 71.7 %shard_map.86 = (bf16[2,8,12288]{2,1,0:T(8,128)(2,1)}, f32[24,2,32,128]{3,2,1,0:T(8,128)}) custom-call(s32[2]{0:T(128)} %bitcast.21, s32[2,24]{1,0:T(2,128)} %bitcast.19, s32[2,24]{1,0:T(2,128)} %bitcast.20, bf16[2,64,12288]{2,1,0:T(8,128)(2,1)} %bitcast.13, bf16[2,64,12288]{2,1,0:T(8,128)(2,1)} %bitcast.14, bf16[2,24,128,128]{3,2,1,0:T(8,128)(2,1)} %bitcast.15, ...), custom_call_target="tpu_custom_call" | custom-call | tf_op jit(solution)/shard_map/pallas_call | solution.py:303
  72.3 1.8 %copy.13 = bf16[2,1,8,12288]{3,2,1,0:T(8,128)(2,1)} copy(bf16[2,1,8,12288]{3,2,1,0:T(8,128)(2,1)} %bitcast.18) | data formatting | bytes 786432
  74.1 2.1 %copy.14 = f32[24,2,1,1,32,128]{5,4,3,2,1,0:T(8,128)} copy(f32[24,2,1,1,32,128]{5,4,3,2,1,0:T(8,128)} %bitcast.17) | data formatting | bytes 1572864

commit v2 on v1

v2 whole, which is shorter than its diff:
```python
import functools

import jax
import jax.numpy as jnp
from jax import lax
from jax.experimental import pallas as pl
from jax.experimental.pallas import tpu as pltpu
from jax.sharding import PartitionSpec as P

MESH = pl.DeviceIdType.MESH
F32 = jnp.float32
BF16 = jnp.bfloat16
ROOT = 0.7978845608028654
CUBIC = 0.044715
PER = 4


def contract(a, b, da, db):
    return lax.dot_general(a, b, (((da,), (db,)), ((), ())), preferred_element_type=F32)


def kernel(
    nz, nmp, groups,
    len_hbm, ii_hbm, io_hbm, x_hbm, g_hbm, wi_hbm, wo_hbm,
    passed_ref, grads_ref,
    len_ref, ii_ref, io_ref,
    x0, x1, g0, g1, wiv, wov, part, from_core, pair, from_x, ready, landed,
    terms, got, code, codes, dx, dx_in,
    in_sem, int_sem, a_send, a_recv, b_send, b_recv, c_send, c_recv,
    t_send, t_recv, k_send, k_recv, d_send, d_recv,
):
    ns = 2 * nz
    size = nz // groups
    chunks = 2 * groups
    s = lax.axis_index("section")
    r = lax.axis_index("dp")
    m = lax.axis_index("mp")
    z, xl = s // 2, lax.rem(s, 2)
    xh, c = r // 2, lax.rem(r, 2)
    rows, width = x0.shape
    count = width // 128
    xs, gs = (x0, x1), (g0, g1)

    def dev(section, dp, mp):
        return {"section": section, "dp": dp, "mp": mp}

    partner = dev(s, 2 * xh + (1 - c), m)
    across = dev(s, 2 * (1 - xh) + c, m)
    sides = [dev(2 * z + (1 - xl), 2 * h + c, m) for h in range(2)]
    down = dev(lax.rem(s + ns - 1, ns), r, m)
    up = dev(lax.rem(s + 1, ns), r, m)

    def spread(me, n, k):
        to = jnp.where(lax.rem(k, 2) == 0, me + (n // 2 - k // 2), me - (n // 2 - (k + 1) // 2))
        return lax.rem(to + n, n)

    def along_z(k):
        return spread(z, nz, k)

    def along_y(k):
        return spread(m, nmp, k)

    ints = [
        pltpu.make_async_copy(ii_hbm, ii_ref, int_sem.at[0]),
        pltpu.make_async_copy(io_hbm, io_ref, int_sem.at[1]),
        pltpu.make_async_copy(len_hbm, len_ref, int_sem.at[2]),
    ]
    for load in ints:
        load.start()
    loads = []
    for p in range(2):
        loads.append([
            pltpu.make_async_copy(x_hbm.at[p], xs[p], in_sem.at[p, 0]),
            pltpu.make_async_copy(wi_hbm.at[p], wiv.at[p], in_sem.at[p, 1]),
            pltpu.make_async_copy(g_hbm.at[p], gs[p], in_sem.at[p, 2]),
            pltpu.make_async_copy(wo_hbm.at[p], wov.at[p], in_sem.at[p, 3]),
        ])
        for load in loads[p]:
            load.start()

    barrier = pltpu.get_barrier_semaphore()

    def greet(target):
        pl.semaphore_signal(barrier, inc=1, device_id=target, device_id_type=MESH)

    @pl.loop(0, nz - 1)
    def _(k):
        greet(dev(2 * along_z(k) + xl, r, m))

    @pl.loop(0, nmp - 1)
    def _(k):
        greet(dev(s, r, along_y(k)))

    for target in [partner, across, sides[0], sides[1], down, up]:
        greet(target)

    for load in ints:
        load.wait()

    wide = code.shape[1]
    lane = lax.broadcasted_iota(jnp.int32, (8, wide), 1)
    relay = lax.broadcasted_iota(jnp.int32, (8, wide), 0)
    value = jnp.full((8, wide), -1, jnp.int32)
    for j in range(2 * nz):
        chosen = jnp.where(relay == 0, ii_ref[0, j], ii_ref[1, j])
        value = jnp.where(lane // 8 == j, chosen * 8 + lane % 8, value)
    code[...] = value

    def compute(n):
        p, g = n // groups, n % groups
        live = lax.broadcasted_iota(jnp.int32, (rows, 128), 0) < len_ref[p]
        for t0 in range(0, size, PER):
            slots = list(range(t0, min(t0 + PER, size)))
            qs = {t: along_z(g * size + t) for t in slots}
            items = [(t, u) for t in slots for u in range(2)]
            x, back, wi, wo, pre, back_pre, act, grad, term = ({} for _ in range(9))
            for i in items:
                j = 2 * qs[i[0]] + i[1]
                x[i] = xs[p][:, pl.ds(ii_ref[p, j] * 128, 128)]
                wi[i] = wiv[p, j]
                pre[i] = contract(x[i], wi[i], 1, 0)
            for i in items:
                j = 2 * qs[i[0]] + i[1]
                picked = gs[p][:, pl.ds(io_ref[p, j] * 128, 128)]
                back[i] = jnp.where(live, picked.astype(F32), 0.0).astype(BF16)
                wo[i] = wov[p, j]
                back_pre[i] = contract(back[i], wo[i], 1, 1)
            for i in items:
                v = pre[i]
                square = v * v
                th = jnp.tanh(ROOT * (v + CUBIC * (square * v)))
                half = 0.5 * (1.0 + th)
                act[i] = (v * half).astype(BF16)
                slope = half + (0.5 * v) * (1.0 - th * th) * (ROOT * (1.0 + (3.0 * CUBIC) * square))
                grad[i] = (back_pre[i] * slope).astype(BF16)
            for i in items:
                t, u = i
                outs = (contract(x[i], grad[i], 0, 0).astype(BF16), contract(act[i], back[i], 0, 0).astype(BF16))
                for kind in range(2):
                    for h in range(2):
                        for d in range(2):
                            lo = 32 * (2 * h + d)
                            part[n, d, u, h, t, kind] = outs[kind][lo:lo + 32]
                term[i] = contract(grad[i], wi[i], 1, 1)
            for t in slots:
                at = pl.multiple_of(16 * qs[t], 16)
                for y in range(nmp):
                    both = jnp.concatenate([term[t, 0][8 * y:8 * y + 8], term[t, 1][8 * y:8 * y + 8]], axis=0)
                    terms[p, y, pl.ds(at, 16), :] = both.astype(BF16)

    def remote(src, dst, send, recv, target):
        return pltpu.make_async_remote_copy(
            src_ref=src, dst_ref=dst, send_sem=send, recv_sem=recv,
            device_id=target, device_id_type=MESH)

    def copy_a(n):
        return remote(part.at[n, 1 - c], from_core.at[n], a_send.at[n], a_recv.at[n], partner)

    def copies_b(n):
        out = [remote(pair.at[n, xl, 1 - xh], from_x.at[n, 0], b_send.at[n, 0], b_recv.at[n, 0], across)]
        for h in range(2):
            out.append(remote(pair.at[n, 1 - xl, h], from_x.at[n, 1 + xh],
                              b_send.at[n, 1 + h], b_recv.at[n, 1 + xh], sides[h]))
        return out

    def copy_c(n, t):
        p, g = n // groups, n % groups
        to = along_z(g * size + t)
        return remote(ready.at[n, t], landed.at[p, z], c_send.at[n, t], c_recv.at[p, z],
                      dev(2 * to + xl, r, m))

    def arrived_c(p, origin):
        return remote(landed.at[p, origin], landed.at[p, origin], c_send.at[0, 0], c_recv.at[p, origin], partner)

    def copy_t(p, to):
        return remote(terms.at[p, to], got.at[p, m], t_send.at[p, to], t_recv.at[p, m], dev(s, r, to))

    def arrived_t(p, origin):
        return remote(got.at[p, origin], got.at[p, origin], t_send.at[p, origin], t_recv.at[p, origin], partner)

    def copy_k(to):
        return remote(code, codes.at[m], k_send.at[to], k_recv.at[m], dev(s, r, to))

    def arrived_k(origin):
        return remote(codes.at[origin], codes.at[origin], k_send.at[origin], k_recv.at[origin], partner)

    def copy_d(p):
        return remote(dx.at[p], dx_in.at[p], d_send.at[p], d_recv.at[p], (down, up)[p])

    def send_terms(p):
        @pl.loop(0, nmp - 1)
        def _(k):
            copy_t(p, along_y(k)).start()
        got[p, m] = terms[p, m]

    def add_pair(n):
        copy_a(n).wait_recv()
        copies = copies_b(n)
        for u in range(2):
            for h in range(2):
                pair[n, u, h] = part[n, c, u, h] + from_core[n, u, h]
        for copy in copies:
            copy.start()

    def add_x(n):
        for i in range(3):
            remote(from_x.at[n, i], from_x.at[n, i], b_send.at[n, i], b_recv.at[n, i], across).wait_recv()
        g = n % groups
        last = size - 1 if g == groups - 1 else size
        for t in range(size):
            ready[n, t, xl] = pair[n, xl, xh, t] + from_x[n, 0, t]
            ready[n, t, 1 - xl] = from_x[n, 1, t] + from_x[n, 2, t]
            if t < last:
                copy_c(n, t).start()
        if g == groups - 1:
            landed[n // groups, z] = ready[n, size - 1]

    def scatter(p):
        first = pl.multiple_of(16 * (m // 2), 16)
        odd = lax.rem(m, 2) == 1
        row = lax.broadcasted_iota(jnp.int32, (8, 128), 0) + 8 * m
        span = 8 * ns
        tile = 8 * count // 3 if (8 * count) % 96 == 0 else 8 * count

        @pl.loop(0, nmp - 1)
        def _(i):
            arrived_t(p, along_y(i)).wait_recv()

        @pl.loop(0, 8 * count // tile)
        def _(i):
            base = i * tile
            place = lax.broadcasted_iota(jnp.int32, (tile, span), 0) + base
            total = jnp.zeros((tile, 128), F32)
            for y in range(nmp):
                hot = (place == codes[y, p:p + 1, :span]).astype(F32).astype(BF16)
                total = total + contract(hot, got[p, y], 1, 0)
            for b in range(tile // 8):
                at = pl.multiple_of(base * 16 + b * 128, 128)
                mine = gs[p][pl.ds(first, 16), pl.ds(at, 128)].astype(F32)
                mine = jnp.where(odd, mine[8:16], mine[0:8])
                mine = jnp.where(row < len_ref[p], mine, 0.0)
                dx[p, :, pl.ds(at, 128)] = (mine + total[8 * b:8 * b + 8]).astype(BF16)
        copy_d(p).start()

    for load in loads[0]:
        load.wait()
    early = min(2, groups)
    for n in range(early):
        compute(n)
    pl.semaphore_wait(barrier, 6 + (nz - 1) + (nmp - 1))
    for n in range(early):
        copy_a(n).start()

    @pl.loop(0, nmp - 1)
    def _(k):
        copy_k(along_y(k)).start()
    codes[m] = code[...]
    if early == groups:
        send_terms(0)
    for n in range(early, chunks):
        if n == groups:
            for load in loads[1]:
                load.wait()
        compute(n)
        copy_a(n).start()
        if n % groups == groups - 1:
            send_terms(n // groups)
        add_pair(n - early)
    moved = 0
    for n in range(chunks - early, chunks):
        add_x(moved)
        moved += 1
        add_pair(n)
    for n in range(moved, chunks):
        add_x(n)

    @pl.loop(0, nmp - 1)
    def _(i):
        arrived_k(along_y(i)).wait_recv()
    for p in range(2):
        scatter(p)

    for n in range(chunks):
        copy_a(n).wait_send()
        for copy in copies_b(n):
            copy.wait_send()

    @pl.loop(0, nmp - 1)
    def _(i):
        copy_k(along_y(i)).wait_send()
        for p in range(2):
            copy_t(p, along_y(i)).wait_send()

    def take(p):
        copy_d(p).wait_recv()
        edge = s == (ns - 1 if p == 0 else 0)
        taken = dx_in[p]
        passed_ref[p] = jnp.where(edge, jnp.zeros_like(taken), taken)

    def total(o):
        q = nz - 1 - o
        for u in range(2):
            for kind in range(2):
                grads_ref[2 * q + u, kind] = (landed[0, q, u, kind].astype(F32)
                                              + landed[1, o, 1 - u, kind].astype(F32))

    @pl.loop(0, nz - 1)
    def _(k):
        arrived_c(0, along_z(k)).wait_recv()
    total(z)
    take(0)

    @pl.loop(0, nz - 1)
    def _(k):
        o = along_z(k)
        arrived_c(1, o).wait_recv()
        total(o)
    take(1)

    for n in range(chunks):
        last = size - 1 if n % groups == groups - 1 else size

        @pl.loop(0, last)
        def _(t):
            copy_c(n, t).wait_send()
    for p in range(2):
        copy_d(p).wait_send()


def body(section_in, out_grad, lengths, w_in, w_out, idx_in, idx_out):
    x = section_in[:, 0]
    g = out_grad[:, 0]
    rows, width = x.shape[1:]
    nf = w_in.shape[2]
    nz = lax.axis_size("section") // 2
    nmp = lax.axis_size("mp")
    wide = -(-8 * nf // 128) * 128
    groups = 3 if nz % 3 == 0 else 1
    chunks, size = 2 * groups, nz // groups
    dma = pltpu.SemaphoreType.DMA
    hbm = pl.BlockSpec(memory_space=pltpu.HBM)
    vmem = pl.BlockSpec(memory_space=pltpu.VMEM)
    slab = (size, 2, 32, 128)
    passed, grads = pl.pallas_call(
        functools.partial(kernel, nz, nmp, groups),
        out_shape=(
            jax.ShapeDtypeStruct((2, 8, width), BF16),
            jax.ShapeDtypeStruct((nf, 2, 32, 128), F32),
        ),
        in_specs=[hbm] * 7,
        out_specs=(vmem, vmem),
        scratch_shapes=[
            pltpu.SMEM((2,), jnp.int32),
            pltpu.SMEM((2, nf), jnp.int32),
            pltpu.SMEM((2, nf), jnp.int32),
            pltpu.VMEM((rows, width), BF16),
            pltpu.VMEM((rows, width), BF16),
            pltpu.VMEM((rows, width), BF16),
            pltpu.VMEM((rows, width), BF16),
            pltpu.VMEM((2, nf, 128, 128), BF16),
            pltpu.VMEM((2, nf, 128, 128), BF16),
            pltpu.VMEM((chunks, 2, 2, 2) + slab, BF16),
            pltpu.VMEM((chunks, 2, 2) + slab, BF16),
            pltpu.VMEM((chunks, 2, 2) + slab, BF16),
            pltpu.VMEM((chunks, 3) + slab, BF16),
            pltpu.VMEM((chunks, size, 2, 2, 32, 128), BF16),
            pltpu.VMEM((2, nz, 2, 2, 32, 128), BF16),
            pltpu.VMEM((2, nmp, 8 * nf, 128), BF16),
            pltpu.VMEM((2, nmp, 8 * nf, 128), BF16),
            pltpu.VMEM((8, wide), jnp.int32),
            pltpu.VMEM((nmp, 8, wide), jnp.int32),
            pltpu.VMEM((2, 8, width), BF16),
            pltpu.VMEM((2, 8, width), BF16),
            dma((2, 4)), dma((3,)), dma((chunks,)), dma((chunks,)), dma((chunks, 3)), dma((chunks, 3)),
            dma((chunks, size)), dma((2, nz)), dma((2, nmp)), dma((2, nmp)),
            dma((nmp,)), dma((nmp,)), dma((2,)), dma((2,)),
        ],
        compiler_params=pltpu.CompilerParams(
            collective_id=0, has_side_effects=True, vmem_limit_bytes=56 * 2**20),
    )(lengths[:, 0, 0], idx_in[0], idx_out[0], x, g, w_in[0], w_out[0])
    return passed[:, None], grads[:, :, None, None]


def solution(mesh):
    placed = (
        P(None, "section", "dp", None),
        P(None, "section", "dp", None),
        P(None, "section", "dp"),
        P("section", None, "mp", None, None),
        P("section", None, "mp", None, None),
        P("section", None, "mp"),
        P("section", None, "mp"),
    )
    return jax.shard_map(
        body,
        mesh=mesh,
        in_specs=placed,
        out_specs=(
            P(None, "section", ("dp", "mp"), None),
            P(None, None, "mp", "section", "dp", None),
        ),
        check_vma=False,
    )
```

time: 76.4 us -> 66.1 us (0.87)
  Pallas kernels: 71.7 us -> 61.4 us
    pallas_call x1, Pallas kernels: 71.7 us -> 61.4 us  [body(): pl.pallas_call(functools.partial(kernel, nz, nmp, groups), out_shape=(jax...]
where the time goes in v2:
time: 66.1 us; the launch traced here: 65.9 us
  Pallas kernels  61.4 us (93%)
  local copies, waits for them, and re-layouts  3.85 us (6%)
    pallas_call x1, Pallas kernels, body(): pl.pallas_call(functools.partial(kernel, nz, nmp, groups), out_shape=(jax...  61.4 us
    unnamed x2, local copies, waits for them, and re-layouts  3.85 us

profile of v2, /device:TPU:1, one launch (start us, length us, event | category | flops | bytes accessed | tf_op | source)
XLA Modules:
  0.0 65.9 jit_solution(6998534509731508796)
XLA Ops:
  0.6 61.4 %shard_map.86 = (bf16[2,8,12288]{2,1,0:T(8,128)(2,1)}, f32[24,2,32,128]{3,2,1,0:T(8,128)}) custom-call(s32[2]{0:T(128)} %bitcast.21, s32[2,24]{1,0:T(2,128)} %bitcast.19, s32[2,24]{1,0:T(2,128)} %bitcast.20, bf16[2,64,12288]{2,1,0:T(8,128)(2,1)} %bitcast.13, bf16[2,64,12288]{2,1,0:T(8,128)(2,1)} %bitcast.14, bf16[2,24,128,128]{3,2,1,0:T(8,128)(2,1)} %bitcast.15, ...), custom_call_target="tpu_custom_call" | custom-call | tf_op jit(solution)/shard_map/pallas_call | solution.py:344
  62.0 1.8 %copy.13 = bf16[2,1,8,12288]{3,2,1,0:T(8,128)(2,1)} copy(bf16[2,1,8,12288]{3,2,1,0:T(8,128)(2,1)} %bitcast.18) | data formatting | bytes 786432
  63.8 2.1 %copy.14 = f32[24,2,1,1,32,128]{5,4,3,2,1,0:T(8,128)} copy(f32[24,2,1,1,32,128]{5,4,3,2,1,0:T(8,128)} %bitcast.17) | data formatting | bytes 1572864

commit v3 on v2

--- a/solution.py
+++ b/solution.py
@@ -13,6 +13,7 @@
 ROOT = 0.7978845608028654
 CUBIC = 0.044715
 PER = 4
+HEAD = 1
 
 
 def contract(a, b, da, db):
@@ -21,13 +22,13 @@
 
 def kernel(
     nz, nmp, groups,
-    len_hbm, ii_hbm, io_hbm, x_hbm, g_hbm, wi_hbm, wo_hbm,
+    tab_hbm, x_hbm, g_hbm, wi_hbm, wo_hbm,
     passed_ref, grads_ref,
-    len_ref, ii_ref, io_ref,
+    tab,
     x0, x1, g0, g1, wiv, wov, part, from_core, pair, from_x, ready, landed,
-    terms, got, code, codes, dx, dx_in,
+    terms, got, code, codes, dx, dx_in, hop,
     in_sem, int_sem, a_send, a_recv, b_send, b_recv, c_send, c_recv,
-    t_send, t_recv, k_send, k_recv, d_send, d_recv,
+    t_send, t_recv, k_send, k_recv, d_send, d_recv, e_send, e_recv, h_send, h_recv, above, above_cross,
 ):
     ns = 2 * nz
     size = nz // groups
@@ -60,13 +61,8 @@
     def along_y(k):
         return spread(m, nmp, k)
 
-    ints = [
-        pltpu.make_async_copy(ii_hbm, ii_ref, int_sem.at[0]),
-        pltpu.make_async_copy(io_hbm, io_ref, int_sem.at[1]),
-        pltpu.make_async_copy(len_hbm, len_ref, int_sem.at[2]),
-    ]
-    for load in ints:
-        load.start()
+    table = pltpu.make_async_copy(tab_hbm, tab, int_sem)
+    table.start()
     loads = []
     for p in range(2):
         loads.append([
@@ -75,53 +71,81 @@
             pltpu.make_async_copy(g_hbm.at[p], gs[p], in_sem.at[p, 2]),
             pltpu.make_async_copy(wo_hbm.at[p], wov.at[p], in_sem.at[p, 3]),
         ])
-        for load in loads[p]:
-            load.start()
+
+    for load in loads[0]:
+        load.start()
 
     barrier = pltpu.get_barrier_semaphore()
 
     def greet(target):
         pl.semaphore_signal(barrier, inc=1, device_id=target, device_id_type=MESH)
 
-    @pl.loop(0, nz - 1)
-    def _(k):
-        greet(dev(2 * along_z(k) + xl, r, m))
+    cross = jnp.where(xl == 0, lax.rem(s + ns - 1, ns), lax.rem(s + 1, ns))
+    cross_above = cross // 2 > z
+
+    def in_column(k):
+        to = along_z(k)
+        return to, dev(2 * to + xl, r, m)
+
+    for target in [partner, across, sides[0], sides[1]]:
+        greet(target)
 
     @pl.loop(0, nmp - 1)
     def _(k):
         greet(dev(s, r, along_y(k)))
 
-    for target in [partner, across, sides[0], sides[1], down, up]:
-        greet(target)
-
-    for load in ints:
-        load.wait()
+    @pl.loop(0, nz - 1)
+    def _(k):
+        to, target = in_column(k)
+
+        @pl.when(to > z)
+        def _():
+            greet(target)
+
+    @pl.when(cross_above)
+    def _():
+        greet(dev(cross, r, m))
+
+    def enter():
+        pl.semaphore_wait(barrier, 4 + (nmp - 1) + z + jnp.where(cross_above, 0, 1))
+
+        @pl.loop(0, nz - 1)
+        def _(k):
+            to, target = in_column(k)
+
+            @pl.when(to < z)
+            def _():
+                pl.semaphore_signal(above.at[z], inc=1, device_id=target, device_id_type=MESH)
+
+        @pl.when(jnp.logical_not(cross_above))
+        def _():
+            pl.semaphore_signal(above_cross, inc=1, device_id=dev(cross, r, m), device_id_type=MESH)
+
+    table.wait()
 
     wide = code.shape[1]
     lane = lax.broadcasted_iota(jnp.int32, (8, wide), 1)
     relay = lax.broadcasted_iota(jnp.int32, (8, wide), 0)
     value = jnp.full((8, wide), -1, jnp.int32)
     for j in range(2 * nz):
-        chosen = jnp.where(relay == 0, ii_ref[0, j], ii_ref[1, j])
+        chosen = jnp.where(relay == 0, tab[0, j] >> 20, tab[1, j] >> 20)
         value = jnp.where(lane // 8 == j, chosen * 8 + lane % 8, value)
     code[...] = value
 
-    def compute(n):
-        p, g = n // groups, n % groups
-        live = lax.broadcasted_iota(jnp.int32, (rows, 128), 0) < len_ref[p]
-        for t0 in range(0, size, PER):
-            slots = list(range(t0, min(t0 + PER, size)))
-            qs = {t: along_z(g * size + t) for t in slots}
+    def compute(p, slots):
+        live = lax.broadcasted_iota(jnp.int32, (rows, 128), 0) < (tab[p, 0] & 255)
+        if slots:
+            qs = {t: along_z(t) for t in slots}
             items = [(t, u) for t in slots for u in range(2)]
             x, back, wi, wo, pre, back_pre, act, grad, term = ({} for _ in range(9))
             for i in items:
                 j = 2 * qs[i[0]] + i[1]
-                x[i] = xs[p][:, pl.ds(ii_ref[p, j] * 128, 128)]
+                x[i] = xs[p][:, pl.ds((tab[p, j] >> 20) * 128, 128)]
                 wi[i] = wiv[p, j]
                 pre[i] = contract(x[i], wi[i], 1, 0)
             for i in items:
                 j = 2 * qs[i[0]] + i[1]
-                picked = gs[p][:, pl.ds(io_ref[p, j] * 128, 128)]
+                picked = gs[p][:, pl.ds(((tab[p, j] >> 8) & 4095) * 128, 128)]
                 back[i] = jnp.where(live, picked.astype(F32), 0.0).astype(BF16)
                 wo[i] = wov[p, j]
                 back_pre[i] = contract(back[i], wo[i], 1, 1)
@@ -140,7 +164,7 @@
                     for h in range(2):
                         for d in range(2):
                             lo = 32 * (2 * h + d)
-                            part[n, d, u, h, t, kind] = outs[kind][lo:lo + 32]
+                            part[p * groups + t // size, d, u, h, t % size, kind] = outs[kind][lo:lo + 32]
                 term[i] = contract(grad[i], wi[i], 1, 1)
             for t in slots:
                 at = pl.multiple_of(16 * qs[t], 16)
@@ -184,8 +208,25 @@
     def arrived_k(origin):
         return remote(codes.at[origin], codes.at[origin], k_send.at[origin], k_recv.at[origin], partner)
 
+    cut = width // 2
+    back_turn = jnp.where(xl == 0, 2, ns - 2)
+    side = dev(2 * z + (1 - xl), r, m)
+    along = dev(lax.rem(s + back_turn, ns), r, m)
+
     def copy_d(p):
-        return remote(dx.at[p], dx_in.at[p], d_send.at[p], d_recv.at[p], (down, up)[p])
+        return remote(dx.at[p, :, :cut], dx_in.at[p, :, :cut], d_send.at[p], d_recv.at[p], (down, up)[p])
+
+    def copy_e():
+        return remote(dx.at[1 - xl, :, cut:], dx_in.at[1 - xl, :, cut:], e_send, e_recv.at[1 - xl], side)
+
+    def copy_hop():
+        return remote(dx.at[xl, :, cut:], hop, h_send.at[0], h_recv, side)
+
+    def forward():
+        return remote(hop, dx_in.at[1 - xl, :, cut:], h_send.at[1], e_recv.at[1 - xl], along)
+
+    def arrived_e(p):
+        return remote(dx_in.at[p, :, cut:], dx_in.at[p, :, cut:], e_send, e_recv.at[p], partner)
 
     def send_terms(p):
         @pl.loop(0, nmp - 1)
@@ -211,6 +252,12 @@
             ready[n, t, xl] = pair[n, xl, xh, t] + from_x[n, 0, t]
             ready[n, t, 1 - xl] = from_x[n, 1, t] + from_x[n, 2, t]
             if t < last:
+                if n < groups:
+                    to = along_z(g * size + t)
+
+                    @pl.when(to > z)
+                    def _():
+                        pl.semaphore_wait(above.at[to], 1)
                 copy_c(n, t).start()
         if g == groups - 1:
             landed[n // groups, z] = ready[n, size - 1]
@@ -238,47 +285,73 @@
                 at = pl.multiple_of(base * 16 + b * 128, 128)
                 mine = gs[p][pl.ds(first, 16), pl.ds(at, 128)].astype(F32)
                 mine = jnp.where(odd, mine[8:16], mine[0:8])
-                mine = jnp.where(row < len_ref[p], mine, 0.0)
+                mine = jnp.where(row < (tab[p, 0] & 255), mine, 0.0)
                 dx[p, :, pl.ds(at, 128)] = (mine + total[8 * b:8 * b + 8]).astype(BF16)
         copy_d(p).start()
 
+    steps = [(p, list(range(t, min(t + PER, nz)))) for p in range(2) for t in range(0, nz, PER)]
+    half = len(steps) // 2
+    early = 1
+
+    def chunks_of(step):
+        p, slots = step
+        return sorted({p * groups + t // size for t in slots})
+
     for load in loads[0]:
         load.wait()
-    early = min(2, groups)
-    for n in range(early):
-        compute(n)
-    pl.semaphore_wait(barrier, 6 + (nz - 1) + (nmp - 1))
-    for n in range(early):
-        copy_a(n).start()
+    for load in loads[1]:
+        load.start()
+    for step in steps[:early]:
+        compute(*step)
+    enter()
+    for step in steps[:early]:
+        for n in chunks_of(step):
+            copy_a(n).start()
 
     @pl.loop(0, nmp - 1)
     def _(k):
         copy_k(along_y(k)).start()
     codes[m] = code[...]
-    if early == groups:
+    if early == half:
         send_terms(0)
-    for n in range(early, chunks):
-        if n == groups:
+    paired = moved = 0
+    for i in range(early, len(steps)):
+        if i == half:
             for load in loads[1]:
                 load.wait()
-        compute(n)
-        copy_a(n).start()
-        if n % groups == groups - 1:
-            send_terms(n // groups)
-        add_pair(n - early)
-    moved = 0
-    for n in range(chunks - early, chunks):
+        if HEAD and i == len(steps) - 1 and i > half:
+            for _ in range(HEAD):
+                add_x(moved)
+                moved += 1
+        compute(*steps[i])
+        for n in chunks_of(steps[i]):
+            copy_a(n).start()
+        if i == half - 1:
+            send_terms(0)
+        while paired <= chunks_of(steps[i - 1])[-1]:
+            add_pair(paired)
+            paired += 1
+    send_terms(1)
+    lead = moved + 1
+    while moved < chunks:
+        if paired < chunks and moved >= lead:
+            add_pair(paired)
+            paired += 1
         add_x(moved)
         moved += 1
-        add_pair(n)
-    for n in range(moved, chunks):
-        add_x(n)
 
     @pl.loop(0, nmp - 1)
     def _(i):
         arrived_k(along_y(i)).wait_recv()
+    @pl.when(cross_above)
+    def _():
+        pl.semaphore_wait(above_cross, 1)
     for p in range(2):
         scatter(p)
+    copy_hop().start()
+    copy_e().start()
+    copy_hop().wait_recv()
+    forward().start()
 
     for n in range(chunks):
         copy_a(n).wait_send()
@@ -293,6 +366,7 @@
 
     def take(p):
         copy_d(p).wait_recv()
+        arrived_e(p).wait_recv()
         edge = s == (ns - 1 if p == 0 else 0)
         taken = dx_in[p]
         passed_ref[p] = jnp.where(edge, jnp.zeros_like(taken), taken)
@@ -325,6 +399,9 @@
             copy_c(n, t).wait_send()
     for p in range(2):
         copy_d(p).wait_send()
+    copy_e().wait_send()
+    copy_hop().wait_send()
+    forward().wait_send()
 
 
 def body(section_in, out_grad, lengths, w_in, w_out, idx_in, idx_out):
@@ -335,23 +412,22 @@
     nz = lax.axis_size("section") // 2
     nmp = lax.axis_size("mp")
     wide = -(-8 * nf // 128) * 128
-    groups = 3 if nz % 3 == 0 else 1
+    groups = 6 if nz % 6 == 0 else 1
     chunks, size = 2 * groups, nz // groups
     dma = pltpu.SemaphoreType.DMA
     hbm = pl.BlockSpec(memory_space=pltpu.HBM)
     vmem = pl.BlockSpec(memory_space=pltpu.VMEM)
     slab = (size, 2, 32, 128)
+    table = (idx_in[0] * 4096 + idx_out[0]) * 256 + lengths[:, 0]
     passed, grads = pl.pallas_call(
         functools.partial(kernel, nz, nmp, groups),
         out_shape=(
             jax.ShapeDtypeStruct((2, 8, width), BF16),
             jax.ShapeDtypeStruct((nf, 2, 32, 128), F32),
         ),
-        in_specs=[hbm] * 7,
+        in_specs=[hbm] * 5,
         out_specs=(vmem, vmem),
         scratch_shapes=[
-            pltpu.SMEM((2,), jnp.int32),
-            pltpu.SMEM((2, nf), jnp.int32),
             pltpu.SMEM((2, nf), jnp.int32),
             pltpu.VMEM((rows, width), BF16),
             pltpu.VMEM((rows, width), BF16),
@@ -371,13 +447,15 @@
             pltpu.VMEM((nmp, 8, wide), jnp.int32),
             pltpu.VMEM((2, 8, width), BF16),
             pltpu.VMEM((2, 8, width), BF16),
-            dma((2, 4)), dma((3,)), dma((chunks,)), dma((chunks,)), dma((chunks, 3)), dma((chunks, 3)),
+            pltpu.VMEM((8, width // 2), BF16),
+            dma((2, 4)), dma, dma((chunks,)), dma((chunks,)), dma((chunks, 3)), dma((chunks, 3)),
             dma((chunks, size)), dma((2, nz)), dma((2, nmp)), dma((2, nmp)),
-            dma((nmp,)), dma((nmp,)), dma((2,)), dma((2,)),
+            dma((nmp,)), dma((nmp,)), dma((2,)), dma((2,)), dma, dma((2,)), dma((2,)), dma,
+            pltpu.SemaphoreType.REGULAR((nz,)), pltpu.SemaphoreType.REGULAR,
         ],
         compiler_params=pltpu.CompilerParams(
-            collective_id=0, has_side_effects=True, vmem_limit_bytes=56 * 2**20),
-    )(lengths[:, 0, 0], idx_in[0], idx_out[0], x, g, w_in[0], w_out[0])
+            collective_id=0, has_side_effects=True, vmem_limit_bytes=52 * 2**20),
+    )(table, x, g, w_in[0], w_out[0])
     return passed[:, None], grads[:, :, None, None]
 
 

time: 66.1 us -> 60.4 us (0.914)
  Pallas kernels: 61.4 us -> 57.2 us
  local copies, waits for them, and re-layouts: 3.85 us -> 1.63 us
  other arithmetic: 0 us -> 0.77 us
    pallas_call x1, Pallas kernels: 61.4 us -> 57.2 us  [body(): pl.pallas_call(functools.partial(kernel, nz, nmp, groups), out_shape=(jax...]
    unnamed x2, local copies, waits for them, and re-layouts: 3.85 us -> 1.63 us
    add x0 -> x1, other arithmetic: none -> 0.77 us  [body(): table = (idx_in[0] * 4096 + idx_out[0]) * 256 + lengths[:, 0]]
where the time goes in v3:
time: 60.4 us; the launch traced here: 60.2 us
  Pallas kernels  57.2 us (95%)
  local copies, waits for them, and re-layouts  1.63 us (3%)
  other arithmetic  0.77 us (1%)
  between operations  0.64 us (1%)
    pallas_call x1, Pallas kernels, body(): pl.pallas_call(functools.partial(kernel, nz, nmp, groups), out_shape=(jax...  57.2 us
    unnamed x2, local copies, waits for them, and re-layouts  1.63 us

profile of v3, /device:TPU:1, one launch (start us, length us, event | category | flops | bytes accessed | tf_op | source)
XLA Modules:
  0.0 60.2 jit_solution(7652937093217527377)
XLA Ops:
  0.6 0.8 %bitcast_add_fusion.tab_hbm = s32[2,24]{1,0:T(2,128)S(1)} fusion(s32[1,2,24]{2,1,0:T(2,128)} %param.13, s32[1,2,24]{2,1,0:T(2,128)} %param.12, s32[2]{0:T(128)} %bitcast.19), kind=kLoop, calls=%fused_computation | loop fusion | flops 192 | bytes 584 | tf_op jit(solution)/shard_map/add | solution.py:421
  1.4 57.2 %shard_map.86 = (bf16[2,8,12288]{2,1,0:T(8,128)(2,1)S(1)}, f32[24,2,32,128]{3,2,1,0:T(8,128)S(1)}) custom-call(s32[2,24]{1,0:T(2,128)S(1)} %bitcast_add_fusion.tab_hbm, bf16[2,64,12288]{2,1,0:T(8,128)(2,1)} %bitcast.15, bf16[2,64,12288]{2,1,0:T(8,128)(2,1)} %bitcast.16, bf16[2,24,128,128]{3,2,1,0:T(8,128)(2,1)} %bitcast.17, bf16[2,24,128,128]{3,2,1,0:T(8,128)(2,1)} %bitcast.18), custom_call_target="tpu_custom_call" | custom-call | tf_op jit(solution)/shard_map/pallas_call | solution.py:422
  58.6 0.7 %copy.13 = bf16[2,1,8,12288]{3,2,1,0:T(8,128)(2,1)} copy(bf16[2,1,8,12288]{3,2,1,0:T(8,128)(2,1)S(1)} %bitcast.14) | data formatting | bytes 786432
  59.3 0.9 %copy.14 = f32[24,2,1,1,32,128]{5,4,3,2,1,0:T(8,128)} copy(f32[24,2,1,1,32,128]{5,4,3,2,1,0:T(8,128)S(1)} %bitcast.13) | data formatting | bytes 1572864

commit v4 on v3

--- a/solution.py
+++ b/solution.py
@@ -209,6 +209,14 @@
         return remote(codes.at[origin], codes.at[origin], k_send.at[origin], k_recv.at[origin], partner)
 
     cut = width // 2
+    ends = jnp.logical_or(s == 0, s == ns - 1)
+    beside = jnp.logical_or(s == 1, s == ns - 2)
+
+    def outward(p):
+        return jnp.logical_not(jnp.logical_and(ends, xl == p))
+
+    def inward(p):
+        return jnp.logical_not(jnp.logical_and(ends, xl == 1 - p))
     back_turn = jnp.where(xl == 0, 2, ns - 2)
     side = dev(2 * z + (1 - xl), r, m)
     along = dev(lax.rem(s + back_turn, ns), r, m)
@@ -287,7 +295,10 @@
                 mine = jnp.where(odd, mine[8:16], mine[0:8])
                 mine = jnp.where(row < (tab[p, 0] & 255), mine, 0.0)
                 dx[p, :, pl.ds(at, 128)] = (mine + total[8 * b:8 * b + 8]).astype(BF16)
-        copy_d(p).start()
+
+        @pl.when(outward(p))
+        def _():
+            copy_d(p).start()
 
     steps = [(p, list(range(t, min(t + PER, nz)))) for p in range(2) for t in range(0, nz, PER)]
     half = len(steps) // 2
@@ -348,10 +359,16 @@
         pl.semaphore_wait(above_cross, 1)
     for p in range(2):
         scatter(p)
-    copy_hop().start()
     copy_e().start()
-    copy_hop().wait_recv()
-    forward().start()
+
+    @pl.when(jnp.logical_not(ends))
+    def _():
+        copy_hop().start()
+
+    @pl.when(jnp.logical_not(beside))
+    def _():
+        copy_hop().wait_recv()
+        forward().start()
 
     for n in range(chunks):
         copy_a(n).wait_send()
@@ -365,11 +382,15 @@
             copy_t(p, along_y(i)).wait_send()
 
     def take(p):
-        copy_d(p).wait_recv()
-        arrived_e(p).wait_recv()
-        edge = s == (ns - 1 if p == 0 else 0)
-        taken = dx_in[p]
-        passed_ref[p] = jnp.where(edge, jnp.zeros_like(taken), taken)
+        @pl.when(inward(p))
+        def _():
+            copy_d(p).wait_recv()
+            arrived_e(p).wait_recv()
+            passed_ref[p] = dx_in[p]
+
+        @pl.when(jnp.logical_not(inward(p)))
+        def _():
+            passed_ref[p] = jnp.zeros(passed_ref.shape[1:], BF16)
 
     def total(o):
         q = nz - 1 - o
@@ -398,10 +419,18 @@
         def _(t):
             copy_c(n, t).wait_send()
     for p in range(2):
-        copy_d(p).wait_send()
+        @pl.when(outward(p))
+        def _():
+            copy_d(p).wait_send()
     copy_e().wait_send()
-    copy_hop().wait_send()
-    forward().wait_send()
+
+    @pl.when(jnp.logical_not(ends))
+    def _():
+        copy_hop().wait_send()
+
+    @pl.when(jnp.logical_not(beside))
+    def _():
+        forward().wait_send()
 
 
 def body(section_in, out_grad, lengths, w_in, w_out, idx_in, idx_out):

time: 60.4 us -> 58.3 us (0.965)
  Pallas kernels: 57.2 us -> 55.1 us
    pallas_call x1, Pallas kernels: 57.2 us -> 55.1 us  [body(): pl.pallas_call(functools.partial(kernel, nz, nmp, groups), out_shape=(jax...]
where the time goes in v4:
time: 58.3 us; the launch traced here: 58.1 us
  Pallas kernels  55.1 us (95%)
  local copies, waits for them, and re-layouts  1.63 us (3%)
  other arithmetic  0.77 us (1%)
  between operations  0.64 us (1%)
    pallas_call x1, Pallas kernels, body(): pl.pallas_call(functools.partial(kernel, nz, nmp, groups), out_shape=(jax...  55.1 us
    unnamed x2, local copies, waits for them, and re-layouts  1.63 us

profile of v4, /device:TPU:1, one launch (start us, length us, event | category | flops | bytes accessed | tf_op | source)
XLA Modules:
  0.0 58.1 jit_solution(11674785037195074474)
XLA Ops:
  0.6 0.8 %bitcast_add_fusion.tab_hbm = s32[2,24]{1,0:T(2,128)S(1)} fusion(s32[1,2,24]{2,1,0:T(2,128)} %param.13, s32[1,2,24]{2,1,0:T(2,128)} %param.12, s32[2]{0:T(128)} %bitcast.19), kind=kLoop, calls=%fused_computation | loop fusion | flops 192 | bytes 584 | tf_op jit(solution)/shard_map/add | solution.py:450
  1.4 55.1 %shard_map.86 = (bf16[2,8,12288]{2,1,0:T(8,128)(2,1)S(1)}, f32[24,2,32,128]{3,2,1,0:T(8,128)S(1)}) custom-call(s32[2,24]{1,0:T(2,128)S(1)} %bitcast_add_fusion.tab_hbm, bf16[2,64,12288]{2,1,0:T(8,128)(2,1)} %bitcast.15, bf16[2,64,12288]{2,1,0:T(8,128)(2,1)} %bitcast.16, bf16[2,24,128,128]{3,2,1,0:T(8,128)(2,1)} %bitcast.17, bf16[2,24,128,128]{3,2,1,0:T(8,128)(2,1)} %bitcast.18), custom_call_target="tpu_custom_call" | custom-call | tf_op jit(solution)/shard_map/pallas_call | solution.py:451
  56.5 0.7 %copy.13 = bf16[2,1,8,12288]{3,2,1,0:T(8,128)(2,1)} copy(bf16[2,1,8,12288]{3,2,1,0:T(8,128)(2,1)S(1)} %bitcast.14) | data formatting | bytes 786432
  57.2 0.9 %copy.14 = f32[24,2,1,1,32,128]{5,4,3,2,1,0:T(8,128)} copy(f32[24,2,1,1,32,128]{5,4,3,2,1,0:T(8,128)S(1)} %bitcast.13) | data formatting | bytes 1572864
